TPU v7x, 256 devices: a whole 4x4x8 slice. The times are simulated.
256 devices in a mesh: req: 64 (over x, y, z_hi), mesh: 4 (over z_lo, core).
Axes of the slice: x: 4, y: 4, z: 8 (z_hi: 4, z_lo: 2; z = z_hi * 2 + z_lo), core: 2. Of those that a mesh axis runs over, the one named last changes fastest.
Arguments:
- tokens: bfloat16 [1024, 64, 1024], P(('req', 'mesh')), may hold values from -6 to 6
- lengths: int32 [1024], P(('req', 'mesh')), may hold values from 1 to 64, 49152 in all
- ridge_keys: float32 [1024, 8, 128, 128], P(('req', 'mesh')), as said below
- ridge_values: float32 [1024, 8, 128, 128], P(('req', 'mesh')), may hold values from -0.5 to 0.5
- conv_tail: bfloat16 [1024, 3, 3072], P(('req', 'mesh')), may hold values from -6 to 6
- page_table: int32 [1024], P(('req', 'mesh')), may hold values from 0 to 15, as said below
- w_qkv: bfloat16 [1024, 3072], P(('req', 'mesh')), may hold values from -0.1875 to 0.1875
- conv_weight: float32 [4, 3072], replicated, may hold values from -3 to 3
- w_gates: bfloat16 [1024, 16], replicated, may hold values from -0.1875 to 0.1875
- decay_rate: float32 [8], replicated, may hold values from 0.001 to 0.03
- ridge: float32 [8], replicated, may hold values from 0.01 to 0.1
- w_out: bfloat16 [1024, 1024], P(('req', 'mesh')), may hold values from -0.1875 to 0.1875
- attn_gain: float32 [1024], replicated, may hold values from 0.5 to 1.5
- ffn_gain: float32 [1024], replicated, may hold values from 0.5 to 1.5
- w_gate: bfloat16 [1024, 2816], P('req', 'mesh'), may hold values from -0.1875 to 0.1875
- w_up: bfloat16 [1024, 2816], P('req', 'mesh'), may hold values from -0.1875 to 0.1875
- w_down: bfloat16 [2816, 1024], P('mesh', 'req'), may hold values from -0.109375 to 0.109375
Outputs:
- mixed: bfloat16 [1024, 64, 1024], P(('req', 'mesh'))
- keys_decode: float32 [1024, 8, 128, 128], P(('req', 'mesh'))
- values_decode: float32 [1024, 8, 128, 128], P(('req', 'mesh'))
- tail_decode: bfloat16 [1024, 3, 3072], P(('req', 'mesh'))
- readout: bfloat16 [1024, 64, 1024], P(('req', 'mesh'))
Inputs may be any that keep to these rules, and one draw needn't show every extreme that they name: `page_table`: within each group of 16 consecutive requests the values are a permutation; value // 4 is a decode device of the group and value % 4 a slot on it, and the 4 requests of one device go to 4 different decode devices. `ridge_keys`: each matrix is symmetric with a positive diagonal that exceeds the sum of the magnitudes of its row's other entries.
All inputs are finite; a program needn't handle non-finite values. No bound on the sum of `lengths` on one device may be relied on, other than what follows from the above.
Results may differ from a plain program's by a relative error of at most 0.0095.
Values may be sent and summed in bfloat16 or wider, within the bound.
A program may use at most 128 MiB of HBM per device.

v0:
```python
import jax
import jax.numpy as jnp
from jax import lax
from jax.sharding import PartitionSpec as P

ITERS = 5


def rms_norm(values, gain):
    return values * lax.rsqrt(jnp.mean(values * values, axis=-1, keepdims=True) + 1e-05) * gain


def unit_rows(values):
    return values * lax.rsqrt(jnp.sum(values * values, axis=-1, keepdims=True) + 1e-06)


def prepare_heads(projected, gate_logits, conv_tail, lengths, conv_weight, decay_rate):
    requests, length, columns = projected.shape
    heads = decay_rate.shape[0]
    window = conv_tail.shape[1]
    extended = jnp.concatenate([conv_tail, projected], axis=1)
    conv_sum = jnp.zeros((requests, length, columns), jnp.float32)
    for tap_index in range(window + 1):
        conv_sum = conv_sum + conv_weight[tap_index] * extended[
            :, tap_index : tap_index + length
        ].astype(jnp.float32)
    activated = jax.nn.silu(conv_sum).reshape(requests, length, 3, heads, columns // (3 * heads))
    queries = unit_rows(activated[:, :, 0])
    keys_now = unit_rows(activated[:, :, 1])
    values_now = activated[:, :, 2]
    position = jnp.arange(length, dtype=jnp.int32)
    live = (position[None, :] < lengths[:, None]).astype(jnp.float32)[:, :, None]
    beta = jax.nn.sigmoid(gate_logits[..., 0]) * live
    log_decay = -decay_rate * jax.nn.softplus(gate_logits[..., 1]) * live
    new_tail = jax.vmap(
        lambda rows_all, first_row: lax.dynamic_slice_in_dim(rows_all, first_row, window, 0)
    )(extended, lengths)
    return (queries, keys_now, values_now, beta, log_decay, new_tail)


def mesa_core(
    queries, keys_now, values_now, beta, log_decay, keys_start, values_start, ridge, iterations
):
    highest = lax.Precision.HIGHEST
    cumulative = jnp.cumsum(jnp.swapaxes(log_decay, 1, 2), axis=-1)
    beta_heads = jnp.swapaxes(beta, 1, 2)
    length = cumulative.shape[-1]
    position = jnp.arange(length, dtype=jnp.int32)
    causal = position[:, None] >= position[None, :]
    spread = cumulative[..., :, None] - cumulative[..., None, :]
    weight = jnp.where(causal, jnp.exp(jnp.minimum(spread, 0.0)), 0.0) * beta_heads[..., None, :]
    carried = jnp.swapaxes(jnp.exp(cumulative), 1, 2)[..., None]
    ridge_term = ridge[None, None, :, None]
    solution = jnp.zeros_like(queries)
    residual = queries
    direction = queries
    res_norm = jnp.sum(residual * residual, axis=-1, keepdims=True)
    for step_index in range(iterations):
        start_part = carried * jnp.einsum(
            "bthj,bhij->bthi", direction, keys_start, precision=highest
        )
        apply_scores = (
            jnp.einsum("bthj,bshj->bhts", direction, keys_now, precision=highest) * weight
        )
        applied = (
            start_part
            + jnp.einsum("bhts,bshj->bthj", apply_scores, keys_now, precision=highest)
            + ridge_term * direction
        )
        step_size = res_norm / (jnp.sum(direction * applied, axis=-1, keepdims=True) + 1e-20)
        solution = solution + step_size * direction
        residual = residual - step_size * applied
        next_norm = jnp.sum(residual * residual, axis=-1, keepdims=True)
        direction = residual + next_norm / (res_norm + 1e-20) * direction
        res_norm = next_norm
    read_start = carried * jnp.einsum("bthj,bhij->bthi", solution, values_start, precision=highest)
    scores = jnp.einsum("bthj,bshj->bhts", solution, keys_now, precision=highest) * weight
    readout = read_start + jnp.einsum("bhts,bshj->bthj", scores, values_now, precision=highest)
    tail_weight = jnp.swapaxes(jnp.exp(cumulative[..., -1:] - cumulative) * beta_heads, 1, 2)[
        ..., None
    ]
    final_decay = jnp.exp(cumulative[..., -1])[..., None, None]
    keys_end = final_decay * keys_start + jnp.einsum(
        "bshi,bshj->bhij", keys_now * tail_weight, keys_now, precision=highest
    )
    values_end = final_decay * values_start + jnp.einsum(
        "bshi,bshj->bhij", values_now * tail_weight, keys_now, precision=highest
    )
    return (readout, keys_end, values_end)


def shards(
    tokens,
    lengths,
    ridge_keys,
    ridge_values,
    conv_tail,
    page_table,
    w_qkv,
    conv_weight,
    w_gates,
    decay_rate,
    ridge,
    w_out,
    attn_gain,
    ffn_gain,
    w_gate,
    w_up,
    w_down,
):
    highest = lax.Precision.HIGHEST
    requests, length, width = tokens.shape
    heads = decay_rate.shape[0]
    row_count = requests * length
    resident = tokens.astype(jnp.float32).reshape(row_count, width)
    normed = rms_norm(resident, attn_gain).astype(jnp.bfloat16)
    columns_in = normed
    projected = jnp.dot(
        columns_in,
        lax.all_gather(w_qkv, ("req", "mesh"), axis=0, tiled=True),
        preferred_element_type=jnp.float32,
    )
    projected = projected.astype(jnp.bfloat16).reshape(requests, length, -1)
    gate_logits = jnp.dot(normed, w_gates, preferred_element_type=jnp.float32).reshape(
        requests, length, heads, 2
    )
    queries, keys_now, values_now, beta, log_decay, new_tail = prepare_heads(
        projected, gate_logits, conv_tail, lengths, conv_weight, decay_rate
    )
    readout, keys_end, values_end = mesa_core(
        queries, keys_now, values_now, beta, log_decay, ridge_keys, ridge_values, ridge, ITERS
    )
    head_rows = readout.reshape(row_count, -1).astype(jnp.bfloat16)
    columns_in = head_rows
    attended = jnp.dot(
        columns_in,
        lax.all_gather(w_out, ("req", "mesh"), axis=0, tiled=True),
        preferred_element_type=jnp.float32,
    )
    after_attn = (resident + attended).astype(jnp.bfloat16)
    ffn_in = rms_norm(after_attn.astype(jnp.float32), ffn_gain).astype(jnp.bfloat16)
    group_tokens = lax.all_gather(ffn_in, "mesh", axis=0, tiled=True)
    columns_in = group_tokens
    gate_proj = jnp.dot(
        columns_in,
        lax.all_gather(w_gate, "req", axis=0, tiled=True),
        preferred_element_type=jnp.float32,
    )
    upward = jnp.dot(
        columns_in,
        lax.all_gather(w_up, "req", axis=0, tiled=True),
        preferred_element_type=jnp.float32,
    )
    hidden = (jax.nn.silu(gate_proj) * upward).astype(jnp.bfloat16)
    down_whole = lax.all_gather(w_down, "req", axis=1, tiled=True)
    ffn_out = lax.psum_scatter(
        jnp.dot(hidden, down_whole, preferred_element_type=jnp.float32).astype(jnp.bfloat16),
        "mesh",
        scatter_dimension=0,
        tiled=True,
    ).astype(jnp.float32)
    mixed = (
        (after_attn.astype(jnp.float32) + ffn_out)
        .astype(jnp.bfloat16)
        .reshape(requests, length, width)
    )
    peers = lax.axis_size("mesh")
    destination = page_table // requests
    slot_index = page_table % requests
    select = (destination[None, :] == jnp.arange(peers, dtype=jnp.int32)[:, None]).astype(
        jnp.float32
    )
    send_keys = jnp.einsum("ej,jhab->ehab", select, keys_end, precision=highest)
    send_values = jnp.einsum("ej,jhab->ehab", select, values_end, precision=highest)
    send_tail = jnp.einsum(
        "ej,jrc->erc", select, new_tail.astype(jnp.float32), precision=highest
    ).astype(jnp.bfloat16)
    send_slot = jnp.sum(jnp.where(select > 0.5, slot_index[None, :], 0), axis=1)
    got_keys, got_values, got_tail, got_slot = (
        lax.all_to_all(
            send_keys.astype(jnp.bfloat16), "mesh", split_axis=0, concat_axis=0, tiled=True
        ).astype(send_keys.dtype),
        lax.all_to_all(
            send_values.astype(jnp.bfloat16), "mesh", split_axis=0, concat_axis=0, tiled=True
        ).astype(send_values.dtype),
        lax.all_to_all(send_tail, "mesh", split_axis=0, concat_axis=0, tiled=True),
        lax.all_to_all(send_slot, "mesh", split_axis=0, concat_axis=0, tiled=True),
    )
    placing = (got_slot[None, :] == jnp.arange(requests, dtype=jnp.int32)[:, None]).astype(
        jnp.float32
    )
    keys_decode = jnp.einsum("si,ihab->shab", placing, got_keys, precision=highest)
    values_decode = jnp.einsum("si,ihab->shab", placing, got_values, precision=highest)
    tail_decode = jnp.einsum(
        "si,irc->src", placing, got_tail.astype(jnp.float32), precision=highest
    ).astype(jnp.bfloat16)
    return (mixed, keys_decode, values_decode, tail_decode, head_rows.reshape(requests, length, -1))


def solution(mesh):
    in_specs = (
        P(("req", "mesh"), None, None),
        P(("req", "mesh")),
        P(("req", "mesh"), None, None, None),
        P(("req", "mesh"), None, None, None),
        P(("req", "mesh"), None, None),
        P(("req", "mesh")),
        P(("req", "mesh"), None),
        P(),
        P(),
        P(),
        P(),
        P(("req", "mesh"), None),
        P(),
        P(),
        P("req", "mesh"),
        P("req", "mesh"),
        P("mesh", "req"),
    )
    out_specs = (
        P(("req", "mesh"), None, None),
        P(("req", "mesh"), None, None, None),
        P(("req", "mesh"), None, None, None),
        P(("req", "mesh"), None, None),
        P(("req", "mesh"), None, None),
    )
    return jax.shard_map(shards, mesh=mesh, in_specs=in_specs, out_specs=out_specs, check_vma=False)
```

profile of v0, /device:TPU:1, one launch (start us, length us, event | category | flops | bytes accessed | tf_op | source)
XLA Modules:
  0.0 583.1 jit_solution(5874164278874121975)
XLA Ops:
  13.0 1.4 fusion.53
  17.6 102.5 %all-gather.19.cloned.1.call-done = bf16[256,4,1024]{2,1,0:T(4,128)(2,1)} async-done(((bf16[1,4,1024]{2,1,0:T(4,128)(2,1)}), bf16[256,4,1024]{2,1,0:T(4,128)(2,1)}) %all-gather.19.cloned.1.call-update) | async-done | bytes 2097168 | tf_op jit(solution)/shard_map/all_gather | solution.py:137
  120.0 3.9 reshape.219
  124.0 114.9 %all-gather.17.cloned.1.call-done = bf16[256,4,3072]{2,1,0:T(4,128)(2,1)} async-done(((bf16[1,4,3072]{2,1,0:T(4,128)(2,1)}), bf16[256,4,3072]{2,1,0:T(4,128)(2,1)}) %all-gather.17.cloned.1.call-update) | async-done | bytes 6291472 | tf_op jit(solution)/shard_map/all_gather | solution.py:120
  238.8 10.7 %reshape.217 = bf16[1024,3072]{1,0:T(8,128)(2,1)} reshape(bf16[256,4,3072]{2,1,0:T(4,128)(2,1)} %all-gather.17.cloned.1.call-done) | data formatting | bytes 12582912
  249.5 4.6 convolution_convert_fusion
  254.1 2.2 divide_multiply_fusion
  259.2 4.1 fusion.30
  263.3 2.2 convolution_multiply_fusion.5
  265.5 2.1 multiply_reduce_fusion.7
  269.9 2.0 convolution_multiply_fusion.4
  271.9 4.1 fusion.27
  276.1 1.7 multiply_reduce_fusion.5
  277.8 1.7 multiply_reduce_fusion.4
  279.9 2.0 convolution_multiply_fusion.3
  281.9 4.1 fusion.24
  286.1 1.7 multiply_reduce_fusion.3
  288.8 2.0 convolution_multiply_fusion.2
  290.8 4.3 fusion.21
  295.1 1.7 multiply_reduce_fusion.1
  298.3 4.2 fusion.18
  302.4 2.0 convolution_multiply_fusion.1
  304.5 1.6 fusion.34
  306.1 2.2 multiply_add_fusion.2
  308.3 2.0 convolution_multiply_fusion
  310.3 4.2 fusion.15
  320.9 3.4 all-to-all-start
  324.7 1.9 pad_maximum_fusion
  326.6 2.5 copy.96
  329.0 1.6 gather_fusion
  330.7 17.5 %all-gather.9.cloned.1.call-done = bf16[1024,1024]{1,0:T(8,128)(2,1)} async-done(((bf16[256,1024]{1,0:T(8,128)(2,1)}), bf16[1024,1024]{1,0:T(8,128)(2,1)}) %all-gather.9.cloned.1.call-update) | async-done | bytes 2097168 | tf_op jit(solution)/shard_map/all_gather | solution.py:142
  348.3 5.3 fusion.107
  353.6 73.4 %all-gather.13.cloned.1.call-done = bf16[1024,704]{1,0:T(8,128)(2,1)} async-done(((bf16[16,704]{1,0:T(8,128)(2,1)}), bf16[1024,704]{1,0:T(8,128)(2,1)}) %all-gather.13.cloned.1.call-update) | async-done | bytes 1441808 | tf_op jit(solution)/shard_map/all_gather | solution.py:151
  426.9 77.3 %all-gather.15.cloned.1.call-done = bf16[704,1024]{0,1:T(8,128)(2,1)} async-done(((bf16[704,16]{0,1:T(8,128)(2,1)}), bf16[704,1024]{0,1:T(8,128)(2,1)}) %all-gather.15.cloned.1.call-update) | async-done | bytes 1441808 | tf_op jit(solution)/shard_map/all_gather | solution.py:155
  504.3 8.2 %convolution_convert_fusion.3 = bf16[1024,1024]{1,0:T(8,128)(2,1)} fusion(bf16[704,1024]{0,1:T(8,128)(2,1)} %all-gather.15.cloned.1.call-done, f32[1024,704]{0,1:T(8,128)} %fusion.107, bf16[1024,1024]{1,0:T(8,128)(2,1)} %all-gather.9.cloned.1.call-done, bf16[1024,704]{1,0:T(8,128)(2,1)} %all-gather.13.cloned.1.call-done), kind=kOutput, calls=%fused_computation.16 | convolution fusion | flops 2958163968 | bytes 9961472 | tf_op jit(solution)/shard_map/dot_general | solution.py:157
  513.3 7.5 %multiply_add_fusion = f32[4,8,128,128]{3,2,1,0:T(8,128)} fusion(f32[4,8,128,128]{3,2,1,0:T(8,128)} %param.20, f32[4,8]{1,0:T(4,128)S(1)} %exp.47, f32[4,64,1,8,128]{4,3,2,1,0:T(8,128)} %copy-done.1, f32[4,64,8]{1,2,0:T(8,128)S(1)} %get-tuple-element.43, f32[4,64,1,8,128]{4,3,2,1,0:T(8,128)S(1)} %get-tuple-element.37, f32[4,64,8]{1,2,0:T(8,128)S(1)} %add_rsqrt_fusion), kind=kOutput, calls=%fused_computation.14 | convolution fusion | flops 404226048 | bytes 6307968 | tf_op jit(solution)/shard_map/bshi,bshj->bhij/dot_general | solution.py:86
  520.8 4.8 all-to-all-start.3
  525.6 4.9 fusion.11
  531.7 4.2 all-to-all-start.2
  535.9 4.7 multiply_add_fusion.1
  540.6 3.3 fusion.8
  545.2 8.5 %all-to-all-done.2 = bf16[4,8,128,128]{3,2,1,0:T(8,128)(2,1)} async-done(((bf16[4,8,128,128]{3,2,1,0:T(8,128)(2,1)}), bf16[4,8,128,128]{3,2,1,0:T(8,128)(2,1)}, u32[]{:S(2)}, u32[]{:S(2)}) %all-to-all-start.2) | async-done | bytes 1048608 | tf_op jit(solution)/shard_map/all_to_all | solution.py:183
  553.7 4.2 all-to-all-start.1
  559.8 2.1 fusion.41
  561.9 1.6 copy.101
  563.5 8.0 %all-to-all-done.1 = bf16[4,8,128,128]{3,2,1,0:T(8,128)(2,1)S(1)} async-done(((bf16[4,8,128,128]{3,2,1,0:T(8,128)(2,1)}), bf16[4,8,128,128]{3,2,1,0:T(8,128)(2,1)S(1)}, u32[]{:S(2)}, u32[]{:S(2)}) %all-to-all-start.1) | async-done | bytes 1048608 | tf_op jit(solution)/shard_map/all_to_all | solution.py:180
  572.4 1.6 copy.100
  574.0 2.0 fusion.38
  (104 shorter events, 29.5 us)
Async XLA Ops:
  7.2 9.4 %copy-start.8 = (bf16[4,64,1024]{2,1,0:T(8,128)(2,1)S(1)}, bf16[4,64,1024]{2,1,0:T(8,128)(2,1)}, u32[]{:S(2)}) copy-start(bf16[4,64,1024]{2,1,0:T(8,128)(2,1)} %param.17) | copy-start | bytes 1572868
  7.2 10.2 %copy-start.11 = (bf16[4,3,3072]{2,0,1:T(4,128)(2,1)S(1)}, bf16[4,3,3072]{2,0,1:T(4,128)(2,1)}, u32[]{:S(2)}) copy-start(bf16[4,3,3072]{2,0,1:T(4,128)(2,1)} %param.21) | copy-start | bytes 221188
  7.2 112.8 %all-gather.19.cloned.1.call-start = ((), (), s32[]{:S(2)}) async-start(), calls=%async_computation.11 | async-start | bytes 2105344 | tf_op jit(solution)/shard_map/all_gather | solution.py:137
  7.9 230.9 %all-gather.17.cloned.1.call-start = ((), (), s32[]{:S(2)}) async-start(), calls=%async_computation.10 | async-start | bytes 6316032 | tf_op jit(solution)/shard_map/all_gather | solution.py:120
  8.7 322.0 %all-gather.11.cloned.1.call-start = ((), (), s32[]{:S(2)}) async-start(), calls=%async_computation.6 | async-start | bytes 1597440 | tf_op jit(solution)/shard_map/all_gather | solution.py:146
  9.4 338.9 %all-gather.9.cloned.1.call-start = ((), (), s32[]{:S(2)}) async-start(), calls=%async_computation.5 | async-start | bytes 2621440 | tf_op jit(solution)/shard_map/all_gather | solution.py:142
  254.1 2.3 copy-start.3
  257.2 57.3 %copy-start.1 = (f32[4,64,1,8,128]{4,3,2,1,0:T(8,128)}, f32[4,64,1,8,128]{4,3,2,1,0:T(8,128)S(1)}, u32[]{:S(2)}) copy-start(f32[4,64,1,8,128]{4,3,2,1,0:T(8,128)S(1)} %get-tuple-element.36) | copy-start | bytes 3145732
  257.2 2.0 copy-start
  263.3 2.2 copy-start.12
  308.2 2.0 copy-start.2
  314.5 1.7 copy-start.9
  314.5 1.8 copy-start.10
  315.8 1.3 copy-start.4
  316.2 1.6 copy-start.13
  316.2 3.8 copy-start.15
  316.2 8.5 %copy-start.14 = (s32[4]{0:T(128)S(1)}, s32[4]{0:T(128)}, u32[]{:S(2)}) copy-start(s32[4]{0:T(128)} %param.18) | copy-start | bytes 52
  317.1 0.8 copy-start.6
  318.9 108.0 %all-gather.13.cloned.1.call-start = ((), (), s32[]{:S(2)}) async-start(), calls=%async_computation.7 | async-start | bytes 1597440 | tf_op jit(solution)/shard_map/all_gather | solution.py:151
  319.5 184.8 %all-gather.15.cloned.1.call-start = ((), (), s32[]{:S(2)}) async-start(), calls=%async_computation.8 | async-start | bytes 1597440 | tf_op jit(solution)/shard_map/all_gather | solution.py:155
  320.9 199.9 %all-to-all-start = ((s32[4,1,1]{2,1,0:T(1,128)}), s32[4,1,1]{2,1,0:T(1,128)S(1)}, u32[]{:S(2)}, u32[]{:S(2)}) async-start(s32[4,1,1]{2,1,0:T(1,128)} %copy.89), calls=%async_computation.1 | async-start | bytes 4096 | tf_op jit(solution)/shard_map/all_to_all | solution.py:187
  324.3 249.7 %reduce-scatter.2.cloned.1.call-start = ((), (), s32[]{:S(2)}) async-start(), calls=%async_computation.9 | async-start | bytes 2621440 | tf_op jit(solution)/shard_map/reduce_scatter | solution.py:156
  520.8 10.9 %all-to-all-start.3 = ((bf16[4,3,3072]{2,1,0:T(4,128)(2,1)}), bf16[4,3,3072]{2,1,0:T(4,128)(2,1)S(1)}, u32[]{:S(2)}, u32[]{:S(2)}) async-start(bf16[4,3,3072]{2,1,0:T(4,128)(2,1)} %copy.97), calls=%async_computation.4 | async-start | bytes 196608 | tf_op jit(solution)/shard_map/all_to_all | solution.py:186
  531.7 22.0 %all-to-all-start.2 = ((bf16[4,8,128,128]{3,2,1,0:T(8,128)(2,1)}), bf16[4,8,128,128]{3,2,1,0:T(8,128)(2,1)}, u32[]{:S(2)}, u32[]{:S(2)}) async-start(bf16[4,8,128,128]{3,2,1,0:T(8,128)(2,1)} %copy.94), calls=%async_computation.3 | async-start | bytes 2097152 | tf_op jit(solution)/shard_map/all_to_all | solution.py:183
  543.9 14.1 %copy-start.5 = (bf16[4,64,8,128]{3,1,2,0:T(8,128)(2,1)S(1)}, bf16[4,64,8,128]{3,1,2,0:T(8,128)(2,1)}, u32[]{:S(2)}) copy-start(bf16[4,64,8,128]{3,1,2,0:T(8,128)(2,1)} %copy-done.4) | copy-start | bytes 1572868
  553.7 17.8 %all-to-all-start.1 = ((bf16[4,8,128,128]{3,2,1,0:T(8,128)(2,1)}), bf16[4,8,128,128]{3,2,1,0:T(8,128)(2,1)S(1)}, u32[]{:S(2)}, u32[]{:S(2)}) async-start(bf16[4,8,128,128]{3,2,1,0:T(8,128)(2,1)} %copy.91), calls=%async_computation.2 | async-start | bytes 2097152 | tf_op jit(solution)/shard_map/all_to_all | solution.py:180
  572.4 1.6 copy-start.7
Sparse Core Ops, SparseCore 0:
  11.8 108.2 all-gather.18
  123.9 114.9 all-gather.16
  242.1 72.7 all-gather.10
  319.0 29.1 all-gather.8
  351.4 75.5 all-gather.12
  430.1 74.1 all-gather.14
  512.6 34.5 reduce-scatter.1
where the time goes:
time: 593 us; the launch traced here: 583 us
  waiting for transfers between devices  405 us (68%)
  matrix products  91.9 us (15%)
  local copies, waits for them, and re-layouts  32 us (5%)
  other arithmetic  21.6 us (4%)
  starting transfers between devices  17.3 us (3%)
  between operations  15 us (3%)
    all_gather x1, waiting for transfers between devices, shards(): lax.all_gather(w_qkv, ('req', 'mesh'), axis=0, tiled=True)  115 us
    all_gather x1, waiting for transfers between devices, shards(): lax.all_gather(w_out, ('req', 'mesh'), axis=0, tiled=True)  102 us
    all_gather x1, waiting for transfers between devices, shards(): down_whole = lax.all_gather(w_down, 'req', axis=1, tiled=True)  77.3 us
    all_gather x1, waiting for transfers between devices, shards(): lax.all_gather(w_up, 'req', axis=0, tiled=True)  73.4 us
    dot_general x5, matrix products, mesa_core(): jnp.einsum('bthj,bhij->bthi', direction, keys_start, precision=highest)  20.8 us
    unnamed x38, local copies, waits for them, and re-layouts  20.7 us
    all_gather x1, waiting for transfers between devices, shards(): group_tokens = lax.all_gather(ffn_in, 'mesh', axis=0, tiled=True)  17.5 us
  transfers between devices with their start and end apart: 11, of which 7 were waited for; matrix products, arithmetic and copies ran while one was open for 24% of the time, Pallas kernels for 0%

commit v1 on v0

v1 whole, which is shorter than its diff:
```python
import functools

import jax
import jax.numpy as jnp
from jax import lax
from jax.experimental import pallas as pl
from jax.experimental.pallas import tpu as pltpu
from jax.sharding import PartitionSpec as P

ITERS = 5
MESH = pl.DeviceIdType.MESH
ANY = pl.BlockSpec(memory_space=pl.ANY)
VMEM = pl.BlockSpec(memory_space=pltpu.VMEM)
NX, NY, NZ, ZH = 4, 4, 8, 4
ALL = None


def place_of():
    req = lax.axis_index("req")
    peer = lax.axis_index("mesh")
    x = req // (NY * ZH)
    y = (req // ZH) % NY
    z = (req % ZH) * 2 + peer // 2
    return x, y, z, peer % 2


def device_of(x, y, z, core):
    return ((x * NY + y) * ZH + z // 2, (z % 2) * 2 + core)


def slab(ref, core, x, y, z, half=None):
    lo, hi = (slice(0, 2), slice(0, ZH)) if z is ALL else (z % 2, z // 2)
    xs = slice(0, NX) if x is ALL else x
    ys = slice(0, NY) if y is ALL else y
    if half is not None:
        if z is ALL:
            lo = slice(half, half + 1)
        else:
            xs = slice(2 * half, 2 * half + 2)
    return ref.at[core, lo, xs, ys, hi]


class Gather:
    def __init__(self, dest, order, sems, base, me):
        self.dest, self.order, self.sems, self.next, self.me = dest, order, sems, base, me
        self.sent = []

    def send(self, where, target):
        x, y, z, core = target
        at = self.next
        self.next += 1
        copy = pltpu.make_async_remote_copy(
            src_ref=where,
            dst_ref=where,
            send_sem=self.sems.at[0, at],
            recv_sem=self.sems.at[1, at],
            device_id=device_of(x, y, z, core),
            device_id_type=MESH,
        )
        copy.start()
        self.sent.append(copy)
        return at

    def arrive(self, where, at):
        pltpu.make_async_remote_copy(
            src_ref=where,
            dst_ref=where,
            send_sem=self.sems.at[0, at],
            recv_sem=self.sems.at[1, at],
            device_id=device_of(*self.me),
            device_id_type=MESH,
        ).wait_recv()

    def moved(self, axis, by):
        place = list(self.me)
        size = (NX, NY, NZ)[axis]
        place[axis] = lax.rem(place[axis] + by + size, size)
        return tuple(place)

    def part(self, axis, by, done, half=None, core=None):
        place = list(self.moved(axis, by))
        for each in done:
            place[each] = ALL
        x, y, z, own = place
        return slab(self.dest, own if core is None else core, x, y, z, half)

    def partner(self):
        x, y, z, core = self.me
        return (x, y, z, 1 - core)

    def stages(self):
        out = []
        first, second, third = self.order
        state = {}

        def direct():
            size = (NX, NY, NZ)[first]
            state["first"] = [
                (by, self.send(self.part(first, 0, ()), self.moved(first, by)))
                for by in range(1, size)
            ]

        def ring(axis, done, last):
            size = (NX, NY, NZ)[axis]
            far = size // 2
            tag = ("ring", axis)

            def cross(by, half):
                if last:
                    at = self.send(self.part(axis, by, done, half), self.partner())
                    state.setdefault("cross", []).append((by, half, at))

            def begin():
                here = self.part(axis, 0, done)
                state[tag] = [
                    (self.send(here, self.moved(axis, 1)), self.send(here, self.moved(axis, -1)))
                ]
                cross(0, None)

            def middle(step):
                right, left = state[tag][-1]
                cut = step == far - 1
                self.arrive(self.part(axis, -step, done), right)
                at_right = self.send(
                    self.part(axis, -step, done, 0 if cut else None), self.moved(axis, 1)
                )
                self.arrive(self.part(axis, step, done), left)
                at_left = self.send(
                    self.part(axis, step, done, 1 if cut else None), self.moved(axis, -1)
                )
                state[tag].append((at_right, at_left))
                cross(-step, None)
                cross(step, None)

            def end():
                right, left = state[tag][-1]
                self.arrive(self.part(axis, far, done, 0), right)
                cross(far, 0)
                self.arrive(self.part(axis, far, done, 1), left)
                cross(far, 1)

            return begin, [functools.partial(middle, s) for s in range(1, far)], end

        b2, m2, e2 = ring(second, (first,), False)
        b3, m3, e3 = ring(third, (first, second), True)

        def after_first():
            for by, at in state["first"]:
                self.arrive(self.part(first, -by, ()), at)
            b2()

        def after_second():
            e2()
            b3()

        def after_cross():
            for by, half, at in state["cross"]:
                self.arrive(
                    self.part(third, by, (first, second), half, core=1 - self.me[3]), at
                )
            for copy in self.sent:
                copy.wait_send()

        out.append(direct)
        out.append(after_first)
        out.extend(m2)
        out.append(after_second)
        out.extend(m3)
        out.append(e3)
        out.append(after_cross)
        return out


COPIES = 26
XYZ, ZYX, ZXY = (0, 1, 2), (2, 1, 0), (2, 0, 1)


def enter(me, group=True):
    barrier = pltpu.get_barrier_semaphore()
    x, y, z, core = me
    others = [(lax.rem(x + by, NX), y, z, core) for by in range(1, NX)]
    others += [(x, lax.rem(y + by, NY), z, core) for by in range(1, NY)]
    others += [(x, y, lax.rem(z + by, NZ), core) for by in range(1, NZ)]
    others += [(x, y, z, 1 - core)]
    if group:
        pair = (z // 2) * 2 + 1 - z % 2
        others += [(x, y, pair, 1 - core)]
    for other in others:
        pl.semaphore_signal(barrier, inc=1, device_id=device_of(*other), device_id_type=MESH)
    pl.semaphore_wait(barrier, len(others))


def run_stages(jobs):
    lists = [job.stages() for job in jobs]
    for step in range(max(len(each) for each in lists)):
        for each in lists:
            if step < len(each):
                each[step]()


def gather_kernel(
    pieces_ref, pages_ref, gate_ref, up_ref, down_ref,
    qa, qb, qc, wo, wg, wu, wd, pages_out,
    landed, rows, stage, sems, group_sems, local_sems,
):
    me = place_of()
    x, y, z, core = me
    req, peer = lax.axis_index("req"), lax.axis_index("mesh")
    enter(me)
    early = []
    for by in range(1, 4):
        other = lax.rem(peer + by, 4)
        for what, (src, dst) in enumerate(
            (
                (pieces_ref.at[other], landed.at[peer]),
                (pages_ref, pages_out.at[peer]),
            )
        ):
            copy = pltpu.make_async_remote_copy(
                src_ref=src,
                dst_ref=dst,
                send_sem=group_sems.at[0, what, by],
                recv_sem=group_sems.at[1, what, by],
                device_id=(req, other),
                device_id_type=MESH,
            )
            copy.start()
            early.append(copy)
    lo, hi = z % 2, z // 2
    own = [
        pltpu.make_async_copy(pages_ref, pages_out.at[peer], local_sems.at[0]),
        pltpu.make_async_copy(gate_ref, wg.at[core, lo, x, y, hi], local_sems.at[1]),
        pltpu.make_async_copy(up_ref, wu.at[core, lo, x, y, hi], local_sems.at[2]),
        pltpu.make_async_copy(down_ref, wd.at[core, lo, x, y, hi], local_sems.at[3]),
        pltpu.make_async_copy(pieces_ref.at[peer], landed.at[peer], local_sems.at[4]),
    ]
    for copy in own:
        copy.start()
    own[4].wait()
    for by in range(1, 4):
        source = lax.rem(peer + 4 - by, 4)
        for what, where in enumerate((landed.at[source], pages_out.at[source])):
            pltpu.make_async_remote_copy(
                src_ref=where,
                dst_ref=where,
                send_sem=group_sems.at[0, what, by],
                recv_sem=group_sems.at[1, what, by],
                device_id=(req, peer),
                device_id_type=MESH,
            ).wait_recv()
    for source in range(4):
        rows[4 * source : 4 * source + 4, :] = landed[source].astype(jnp.float32)
    stage[...] = rows[...].astype(jnp.bfloat16)
    blocks = [
        pltpu.make_async_copy(
            stage.at[:, 256 * n : 256 * n + 256],
            ref.at[core, lo, x, y, hi],
            local_sems.at[5 + n],
        )
        for n, ref in enumerate((qa, qb, qc, wo))
    ]
    for copy in blocks:
        copy.start()
    for copy in blocks:
        copy.wait()
    for copy in own[:4]:
        copy.wait()
    run_stages(
        [
            Gather(ref, order, sems.at[n], 0, me)
            for n, (ref, order) in enumerate(
                (
                    (qa, XYZ), (qb, ZYX), (qc, ZXY), (wg, XYZ), (wu, ZYX), (wd, ZXY), (wo, ZXY),
                )
            )
        ]
    )
    for copy in early:
        copy.wait_send()


def gather_all(pieces, pages, gate, up, down):
    grid = (2, 2, NX, NY, ZH, 16)

    def block(n):
        return jax.ShapeDtypeStruct(grid + (n,), jnp.bfloat16)

    ff = gate.shape[1]
    return pl.pallas_call(
        gather_kernel,
        name="gather_weights",
        out_shape=[block(256)] * 4
        + [block(ff)] * 3
        + [jax.ShapeDtypeStruct((4,) + pages.shape, jnp.int32)],
        in_specs=[VMEM] * 5,
        out_specs=[ANY] * 8,
        scratch_shapes=[
            pltpu.VMEM((4, 4, 1024), jnp.bfloat16),
            pltpu.VMEM((16, 1024), jnp.float32),
            pltpu.VMEM((16, 1024), jnp.bfloat16),
            pltpu.SemaphoreType.DMA((7, 2, COPIES)),
            pltpu.SemaphoreType.DMA((2, 2, 4)),
            pltpu.SemaphoreType.DMA((9,)),
        ],
        compiler_params=pltpu.CompilerParams(collective_id=0, has_side_effects=True),
    )(pieces, pages, gate, up, down)


def split2(value):
    high = value.astype(jnp.bfloat16)
    low = (value - high.astype(jnp.float32)).astype(jnp.bfloat16)
    return jnp.concatenate([high, low], axis=0)


def dot(a, b, contract=((1,), (0,)), precision=None):
    return lax.dot_general(
        a, b, (contract, ((), ())), preferred_element_type=jnp.float32, precision=precision
    )


def dot2(stacked, b, contract=((1,), (0,))):
    both = dot(stacked, b, contract)
    half = both.shape[0] // 2
    return both[:half] + both[half:]


def rms_norm(values, gain):
    return values * lax.rsqrt(jnp.mean(values * values, axis=-1, keepdims=True) + 1e-05) * gain


def mesa_kernel(
    lengths, dest, ridge,
    tokens, w_gates, gain, rate, rate_col, conv_weight, tail, keys0, values0, qa, qb, qc,
    readout, send_keys, send_values, send_tail,
    normed, projected, extended, act,
):
    r = pl.program_id(0)
    high = lax.Precision.HIGHEST

    @pl.when(r == 0)
    def _():
        normed[...] = rms_norm(tokens[...].astype(jnp.float32), gain[...]).astype(jnp.bfloat16)
        for core in range(2):
            for lo in range(2):
                for n, ref in enumerate((qa, qb, qc)):
                    at = (lo * 2 + core) * 768 + n * 256
                    projected[:, at : at + 256] = dot(
                        normed[...], ref[core * 2 + lo]
                    ).astype(jnp.bfloat16)

    length = lengths[r]
    mine = pl.ds(pl.multiple_of(r * 64, 64), 64)
    extended[5:8, :] = tail[0].astype(jnp.float32)
    extended[8:72, :] = projected[mine, :].astype(jnp.float32)
    from_row = 5 + length
    window = extended[pl.ds(pl.multiple_of(from_row // 8 * 8, 8), 16), :]
    send_tail[0] = pltpu.roll(window, (16 - from_row % 8) % 16, 0)[:3].astype(jnp.bfloat16)
    total = conv_weight[0:1, :] * extended[5:69, :]
    for tap in range(1, 4):
        total = total + conv_weight[tap : tap + 1, :] * extended[5 + tap : 69 + tap, :]
    act[...] = total * jax.nn.sigmoid(total)

    logits = dot(normed[mine, :], w_gates[...])
    pick_row = lax.broadcasted_iota(jnp.int32, (16, 8), 0)
    pick_col = lax.broadcasted_iota(jnp.int32, (16, 8), 1)
    in_logit = dot(logits, (pick_row == 2 * pick_col).astype(jnp.float32), precision=high)
    out_logit = dot(logits, (pick_row == 2 * pick_col + 1).astype(jnp.float32), precision=high)
    slot = lax.broadcasted_iota(jnp.int32, (64, 8), 0)
    live = (slot < length).astype(jnp.float32)
    beta = jax.nn.sigmoid(in_logit) * live
    log_decay = -rate[...] * jax.nn.softplus(out_logit) * live
    t_at = lax.broadcasted_iota(jnp.int32, (64, 64), 0)
    s_at = lax.broadcasted_iota(jnp.int32, (64, 64), 1)
    causal = s_at <= t_at
    lower = causal.astype(jnp.float32)
    same = (t_at == s_at).astype(jnp.float32)
    cum = dot(lower, log_decay, precision=high)
    cum_rows = dot(cum, same, ((0,), (0,)), precision=high)
    beta_rows = dot(beta, same, ((0,), (0,)), precision=high)
    carried_all = jnp.exp(cum)

    for first in range(0, 8, HEADS_AT_ONCE):
        heads = range(first, first + HEADS_AT_ONCE)
        states = []
        for h in heads:
            q = act[:, h * 128 : h * 128 + 128]
            k = act[:, 1024 + h * 128 : 1152 + h * 128]
            v = act[:, 2048 + h * 128 : 2176 + h * 128]
            q = q * lax.rsqrt(jnp.sum(q * q, axis=-1, keepdims=True) + 1e-06)
            k = k * lax.rsqrt(jnp.sum(k * k, axis=-1, keepdims=True) + 1e-06)
            cum_col, cum_row = cum[:, h : h + 1], cum_rows[h : h + 1, :]
            beta_row = beta_rows[h : h + 1, :]
            spread = jnp.exp(jnp.minimum(cum_col - cum_row, 0.0))
            weight = jnp.where(causal, spread, 0.0) * beta_row
            last = cum[63:64, h : h + 1]
            final = jnp.exp(last)
            tail_row = jnp.exp(last - cum_row) * beta_row
            k_b = k.astype(jnp.bfloat16)
            k_t, v_t = k.T, v.T
            start_k, start_v = keys0[0, h], values0[0, h]
            send_keys[0, h] = (
                final * start_k + dot2(split2(k_t * tail_row), k_b)
            ).astype(jnp.bfloat16)
            send_values[0, h] = (
                final * start_v + dot2(split2(v_t * tail_row), k_b)
            ).astype(jnp.bfloat16)
            right = jnp.concatenate(
                [start_k.astype(jnp.bfloat16), k_t.astype(jnp.bfloat16)], axis=1
            )
            states.append(
                dict(
                    x=jnp.zeros_like(q), res=q, p=q, rr=jnp.sum(q * q, axis=-1, keepdims=True),
                    right=right, k_b=k_b, k_tb=k_t.astype(jnp.bfloat16), v_b=v.astype(jnp.bfloat16),
                    v0=start_v.astype(jnp.bfloat16), weight=weight,
                    carried=carried_all[:, h : h + 1], ridge=ridge[h],
                )
            )
        for _ in range(ITERS):
            for s in states:
                both = dot2(split2(s["p"]), s["right"])
                s["start"] = s["carried"] * both[:, :128]
                s["scores"] = both[:, 128:] * s["weight"]
            for s in states:
                applied = (
                    s["start"] + dot2(split2(s["scores"]), s["k_b"]) + s["ridge"] * s["p"]
                )
                step = s["rr"] / (jnp.sum(s["p"] * applied, axis=-1, keepdims=True) + 1e-20)
                s["x"] = s["x"] + step * s["p"]
                s["res"] = s["res"] - step * applied
                after = jnp.sum(s["res"] * s["res"], axis=-1, keepdims=True)
                s["p"] = s["res"] + after / (s["rr"] + 1e-20) * s["p"]
                s["rr"] = after
        for h, s in zip(heads, states):
            stacked = split2(s["x"])
            start = s["carried"] * dot2(stacked, s["v0"], ((1,), (1,)))
            scores = dot2(stacked, s["k_tb"]) * s["weight"]
            readout[:, h * 128 : h * 128 + 128] = (
                start + dot2(split2(scores), s["v_b"])
            ).astype(jnp.bfloat16)


HEADS_AT_ONCE = 4


def mesa(lengths, dest, ridge, tokens, w_gates, gain, rate, conv_weight, tail, keys0, values0, qs):
    def whole(shape):
        return pl.BlockSpec(shape, lambda r, *_: (0,) * len(shape))

    def by_request(shape):
        return pl.BlockSpec(shape, lambda r, *_: (r,) + (0,) * (len(shape) - 1))

    def by_dest(shape):
        return pl.BlockSpec(shape, lambda r, n, d, *_: (d[r],) + (0,) * (len(shape) - 1))

    state = (1, 8, 128, 128)
    return pl.pallas_call(
        mesa_kernel,
        name="mesa",
        grid_spec=pltpu.PrefetchScalarGridSpec(
            num_scalar_prefetch=3,
            grid=(4,),
            in_specs=[
                whole((256, 1024)), whole((1024, 16)), whole((1, 1024)), whole((1, 8)),
                whole((8, 1)), whole((4, 3072)), by_request((1, 3, 3072)), by_request(state),
                by_request(state), whole((4, 1024, 256)), whole((4, 1024, 256)),
                whole((4, 1024, 256)),
            ],
            out_specs=[
                by_request((64, 1024)), by_dest(state), by_dest(state), by_dest((1, 3, 3072)),
            ],
            scratch_shapes=[
                pltpu.VMEM((256, 1024), jnp.bfloat16),
                pltpu.VMEM((256, 3072), jnp.bfloat16),
                pltpu.VMEM((80, 3072), jnp.float32),
                pltpu.VMEM((64, 3072), jnp.float32),
            ],
        ),
        out_shape=[
            jax.ShapeDtypeStruct((256, 1024), jnp.bfloat16),
            jax.ShapeDtypeStruct((4, 8, 128, 128), jnp.bfloat16),
            jax.ShapeDtypeStruct((4, 8, 128, 128), jnp.bfloat16),
            jax.ShapeDtypeStruct((4, 3, 3072), jnp.bfloat16),
        ],
        compiler_params=pltpu.CompilerParams(vmem_limit_bytes=60 << 20),
    )(
        lengths, dest, ridge, tokens, w_gates, gain, rate, rate.reshape(8, 1), conv_weight, tail,
        keys0, values0, *qs,
    )


def handover_kernel(keys, values, tails, got_keys, got_values, got_tails, sems):
    req, peer = lax.axis_index("req"), lax.axis_index("mesh")
    barrier = pltpu.get_barrier_semaphore()
    for by in range(1, 4):
        pl.semaphore_signal(
            barrier, inc=1, device_id=(req, lax.rem(peer + by, 4)), device_id_type=MESH
        )
    pl.semaphore_wait(barrier, 3)
    copies = []
    for by in range(1, 4):
        other = lax.rem(peer + by, 4)
        for n, (src, dst) in enumerate(
            ((keys, got_keys), (values, got_values), (tails, got_tails))
        ):
            copy = pltpu.make_async_remote_copy(
                src_ref=src.at[other],
                dst_ref=dst.at[peer],
                send_sem=sems.at[0, by, n],
                recv_sem=sems.at[1, by, n],
                device_id=(req, other),
                device_id_type=MESH,
            )
            copy.start()
            copies.append(copy)
    for by in range(1, 4):
        source = lax.rem(peer + 4 - by, 4)
        for n, dst in enumerate((got_keys, got_values, got_tails)):
            pltpu.make_async_remote_copy(
                src_ref=dst.at[source],
                dst_ref=dst.at[source],
                send_sem=sems.at[0, by, n],
                recv_sem=sems.at[1, by, n],
                device_id=(req, peer),
                device_id_type=MESH,
            ).wait_recv()
    for copy in copies:
        copy.wait_send()


def handover(keys, values, tails):
    return pl.pallas_call(
        handover_kernel,
        name="handover",
        out_shape=[jax.ShapeDtypeStruct(a.shape, a.dtype) for a in (keys, values, tails)],
        in_specs=[ANY] * 3,
        out_specs=[ANY] * 3,
        scratch_shapes=[pltpu.SemaphoreType.DMA((2, 4, 3))],
        compiler_params=pltpu.CompilerParams(collective_id=1, has_side_effects=True),
    )(keys, values, tails)


def finish_kernel(
    slots, me,
    readout, tokens, gain, w_out, w_gate, w_up, w_down,
    got_keys, got_values, got_tails, own_keys, own_values, own_tails,
    mixed, keys, values, tails,
    after, ffn_in, total,
):
    q = pl.program_id(0)

    @pl.when(q == 0)
    def _():
        for core in range(2):
            for lo in range(2):
                at = (lo * 2 + core) * 256
                after[:, at : at + 256] = (
                    tokens[:, at : at + 256].astype(jnp.float32)
                    + dot(readout[...], w_out[core * 2 + lo])
                ).astype(jnp.bfloat16).astype(jnp.float32)
        ffn_in[...] = rms_norm(after[...], gain[...]).astype(jnp.bfloat16)

    gate = dot(ffn_in[...], w_gate[0])
    hidden = (gate * jax.nn.sigmoid(gate) * dot(ffn_in[...], w_up[0])).astype(jnp.bfloat16)
    part = dot(hidden, w_down[0], ((1,), (1,)))

    @pl.when(q == 0)
    def _():
        total[...] = part

    @pl.when(jnp.logical_and(q > 0, q < 3))
    def _():
        total[...] += part

    @pl.when(q == 3)
    def _():
        mixed[...] = (after[...] + (total[...] + part)).astype(jnp.bfloat16)

    mine = me[0] == q
    keys[...] = jnp.where(mine, own_keys[...], got_keys[...]).astype(jnp.float32)
    values[...] = jnp.where(mine, own_values[...], got_values[...]).astype(jnp.float32)
    tails[...] = jnp.where(mine, own_tails[...], got_tails[...])


def finish(slots, me, readout, tokens, gain, w_out, w_gate, w_up, w_down, got, own):
    def whole(shape):
        return pl.BlockSpec(shape, lambda q, *_: (0,) * len(shape))

    def by_step(shape):
        return pl.BlockSpec(shape, lambda q, *_: (q,) + (0,) * (len(shape) - 1))

    def mine(shape):
        return pl.BlockSpec(shape, lambda q, s, m: (m[0],) + (0,) * (len(shape) - 1))

    def by_slot(shape):
        return pl.BlockSpec(shape, lambda q, s, m: (s[q],) + (0,) * (len(shape) - 1))

    state, tail = (1, 8, 128, 128), (1, 3, 3072)
    ff = w_gate.shape[-1]
    return pl.pallas_call(
        finish_kernel,
        name="finish",
        grid_spec=pltpu.PrefetchScalarGridSpec(
            num_scalar_prefetch=2,
            grid=(4,),
            in_specs=[
                whole((256, 1024)), whole((256, 1024)), whole((1, 1024)), whole((4, 1024, 256)),
                by_step((1, 1024, ff)), by_step((1, 1024, ff)), by_step((1, 1024, ff)),
                by_step(state), by_step(state), by_step(tail),
                mine(state), mine(state), mine(tail),
            ],
            out_specs=[whole((256, 1024)), by_slot(state), by_slot(state), by_slot(tail)],
            scratch_shapes=[
                pltpu.VMEM((256, 1024), jnp.float32),
                pltpu.VMEM((256, 1024), jnp.bfloat16),
                pltpu.VMEM((256, 1024), jnp.float32),
            ],
        ),
        out_shape=[
            jax.ShapeDtypeStruct((256, 1024), jnp.bfloat16),
            jax.ShapeDtypeStruct((4, 8, 128, 128), jnp.float32),
            jax.ShapeDtypeStruct((4, 8, 128, 128), jnp.float32),
            jax.ShapeDtypeStruct((4, 3, 3072), jnp.bfloat16),
        ],
        compiler_params=pltpu.CompilerParams(vmem_limit_bytes=60 << 20),
    )(slots, me, readout, tokens, gain, w_out, w_gate, w_up, w_down, *got, *own)


def shards(
    tokens, lengths, ridge_keys, ridge_values, conv_tail, page_table, w_qkv, conv_weight, w_gates,
    decay_rate, ridge, w_out, attn_gain, ffn_gain, w_gate, w_up, w_down,
):
    requests, length, width = tokens.shape
    flat = tokens.reshape(requests * length, width)
    pieces = jnp.concatenate(
        [w_qkv.reshape(4, 4, 768).swapaxes(0, 1), w_out.reshape(4, 4, 256).swapaxes(0, 1)], axis=2
    )
    pages = jnp.broadcast_to(page_table[None, :], (8, requests))
    pages = jnp.pad(pages, ((0, 0), (0, 128 - requests)))
    *weights, all_pages = gather_all(pieces, pages, w_gate, w_up, w_down.T)
    qa, qb, qc, wo, wg, wu, wd = [w.reshape(4, 1024, w.shape[-1]) for w in weights]
    me = lax.axis_index("mesh").astype(jnp.int32)
    group = all_pages[:, 0, :requests]
    slots = jnp.sum(jnp.where(group // requests == me, group % requests, 0), axis=1)
    readout, *own = mesa(
        lengths, page_table // requests, ridge, flat, w_gates, attn_gain[None, :],
        decay_rate[None, :], conv_weight, conv_tail, ridge_keys, ridge_values, (qa, qb, qc),
    )
    got = handover(*own)
    mixed, keys, values, tails = finish(
        slots, me[None], readout, flat, ffn_gain[None, :], wo, wg, wu, wd, got, own
    )
    return (
        mixed.reshape(tokens.shape), keys, values, tails, readout.reshape(requests, length, -1)
    )


def solution(mesh):
    both = ("req", "mesh")
    in_specs = (
        P(both, None, None), P(both), P(both, None, None, None), P(both, None, None, None),
        P(both, None, None), P(both), P(both, None), P(), P(), P(), P(), P(both, None), P(), P(),
        P("req", "mesh"), P("req", "mesh"), P("mesh", "req"),
    )
    out_specs = (
        P(both, None, None), P(both, None, None, None), P(both, None, None, None),
        P(both, None, None), P(both, None, None),
    )
    return jax.shard_map(shards, mesh=mesh, in_specs=in_specs, out_specs=out_specs, check_vma=False)
```

time: 593 us -> 184 us (0.31); the launches traced: 583 us -> 184 us
  waiting for transfers between devices: 405 us -> 0 us
  Pallas kernels: 0 us -> 172 us
  matrix products: 91.9 us -> 0 us
  local copies, waits for them, and re-layouts: 32 us -> 8.04 us
  other arithmetic: 21.6 us -> 3.2 us
  starting transfers between devices: 17.3 us -> 0 us
  between operations: 15 us -> 0.66 us
    all_gather x6 -> x0, waiting for transfers between devices: 386 us -> none  [the longest x1 115 us: shards(): lax.all_gather(w_qkv, ('req', 'mesh'), axis=0, tiled=True)]
    pallas_call x0 -> x4, Pallas kernels: none -> 172 us  [the longest x1 94.8 us: gather_all(): pl.pallas_call(gather_kernel, name='gather_weights', out_shape=[block(256...]
    dot_general x31 -> x0, matrix products: 91.9 us -> none  [the longest x5 20.8 us: mesa_core(): jnp.einsum('bthj,bhij->bthi', direction, keys_start, precision=highest)]
    all_to_all x4 -> x0, starting transfers between devices: 16.6 us -> none  [the longest x1 4.76 us: shards(): lax.all_to_all(send_tail, 'mesh', split_axis=0, concat_axis=0, tiled=True)]
    all_to_all x4 -> x0, waiting for transfers between devices: 16.5 us -> none  [the longest x1 8.52 us: shards(): lax.all_to_all(send_values.astype(jnp.bfloat16), 'mesh', split_axis=0, co...]
    unnamed x38 -> x3, local copies, waits for them, and re-layouts: 20.7 us -> 4.74 us
  transfers between devices with their start and end apart: 11 -> 0, of which waited for: 7 -> 0; matrix products, arithmetic and copies ran while one was open for 24% -> 0% of each run, Pallas kernels for 0% -> 0%
where the time goes in v1:
time: 184 us
  Pallas kernels  172 us (93%)
  local copies, waits for them, and re-layouts  8.04 us (4%)
  other arithmetic  3.2 us (2%)
    pallas_call x1, Pallas kernels, gather_all(): pl.pallas_call(gather_kernel, name='gather_weights', out_shape=[block(256...  94.8 us
    pallas_call x1, Pallas kernels, mesa(): pl.pallas_call(mesa_kernel, name='mesa', grid_spec=pltpu.PrefetchScalarGr...  35.1 us
    pallas_call x1, Pallas kernels, handover(): pl.pallas_call(handover_kernel, name='handover', out_shape=[jax.ShapeDtyp...  26.7 us
    pallas_call x1, Pallas kernels, finish(): pl.pallas_call(finish_kernel, name='finish', grid_spec=pltpu.PrefetchScal...  15 us
    unnamed x3, local copies, waits for them, and re-layouts  4.74 us

profile of v1, /device:TPU:1, one launch (start us, length us, event | category | flops | bytes accessed | tf_op | source)
XLA Modules:
  0.0 183.6 jit_solution(5753342689548560867)
XLA Ops:
  0.6 0.7 pad.6
  1.3 1.2 and_select_fusion.dest
  2.5 0.6 pad.7.pages_ref
  3.1 1.3 copy.23.rate_col
  4.4 1.4 pad_maximum_fusion.pieces_ref
  5.8 1.6 copy.24.tail
  7.4 1.6 copy.22.w_gates
  8.9 94.8 %gather_weights.1 = (bf16[2,2,4,4,4,16,256]{6,5,4,3,2,1,0:T(8,128)(2,1)}, bf16[2,2,4,4,4,16,256]{6,5,4,3,2,1,0:T(8,128)(2,1)}, bf16[2,2,4,4,4,16,256]{6,5,4,3,2,...) custom-call(bf16[4,4,1024]{2,1,0:T(4,128)(2,1)} %pad_maximum_fusion., ...), custom_call_target="tpu_custom_call" | custom-call | tf_op jit(solution)/shard_map/gather_weights/pallas_call | solution.py:289
  103.8 0.7 slice.3
  104.5 0.6 fusion.2.slots
  105.1 35.1 %mesa.1 = (bf16[256,1024]{1,0:T(8,128)(2,1)}, bf16[4,8,128,128]{3,2,1,0:T(8,128)(2,1)}, bf16[4,8,128,128]{3,2,1,0:T(8,128)(2,1)}, bf16[4,3,3072]{2,1,0:T(4,128)(2,1)}) custom-call(s32[4]{0:T(128)} %lengths.1, s32[4]{0:T(128)} %and_select_fusion.dest, f32[8]{0:T(128)} %ridge.1, bf16[256,1024]{1,0:T(8,128)(2,1)} %bitcast.30, bf16[1024,16]{1,0:T(8,128)(2,1)} %copy.22.w_gates, ...), custom_call_target="tpu_custom_call" | custom-call | tf_op jit(solution)/shard_map/mesa/pallas_call | solution.py:456
  140.3 26.7 %handover.1 = (bf16[4,8,128,128]{3,2,1,0:T(8,128)(2,1)}, bf16[4,8,128,128]{3,2,1,0:T(8,128)(2,1)}, bf16[4,3,3072]{2,1,0:T(4,128)(2,1)}) custom-call(bf16[4,8,128,128]{3,2,1,0:T(8,128)(2,1)} %get-tuple-element.33.keys.own_keys, bf16[4,8,128,128]{3,2,1,0:T(8,128)(2,1)} %get-tuple-element.34.values.own_values, bf16[4,3,3072]{2,1,0:T(4,128)(2,1)} %get-tuple-element.35.tails.own_tails), custom_call_target="tpu_custom_call" | custom-call | tf_op jit(solution)/shard_map/handover/pallas_call | solution.py:531
  167.0 15.0 %finish.1 = (bf16[256,1024]{1,0:T(8,128)(2,1)}, f32[4,8,128,128]{3,2,1,0:T(8,128)}, f32[4,8,128,128]{3,2,1,0:T(8,128)}, bf16[4,3,3072]{2,1,0:T(4,128)(2,1)}) custom-call(s32[4]{0:T(128)} %fusion.2.slots, s32[1]{0:T(128)} %bitcast.6.me, bf16[256,1024]{1,0:T(8,128)(2,1)} %get-tuple-element.28.readout, bf16[256,1024]{1,0:T(8,128)(2,1)} %bitcast.31, ...), custom_call_target="tpu_custom_call" | custom-call | tf_op jit(solution)/shard_map/finish/pallas_call | solution.py:599
  182.0 1.6 copy.25

commit v2 on v1

--- a/solution.py
+++ b/solution.py
@@ -328,11 +328,11 @@
     return values * lax.rsqrt(jnp.mean(values * values, axis=-1, keepdims=True) + 1e-05) * gain
 
 
-def mesa_kernel(
-    lengths, dest, ridge,
-    tokens, w_gates, gain, rate, rate_col, conv_weight, tail, keys0, values0, qa, qb, qc,
-    readout, send_keys, send_values, send_tail,
-    normed, projected, extended, act,
+def statistics_kernel(
+    lengths, dest,
+    tokens, w_gates, gain, rate, conv_weight, tail, keys0, values0, qa, qb, qc,
+    act, sums, rows, send_keys, send_values, send_tail,
+    normed, projected, extended,
 ):
     r = pl.program_id(0)
     high = lax.Precision.HIGHEST
@@ -371,14 +371,128 @@
     log_decay = -rate[...] * jax.nn.softplus(out_logit) * live
     t_at = lax.broadcasted_iota(jnp.int32, (64, 64), 0)
     s_at = lax.broadcasted_iota(jnp.int32, (64, 64), 1)
-    causal = s_at <= t_at
-    lower = causal.astype(jnp.float32)
+    lower = (s_at <= t_at).astype(jnp.float32)
     same = (t_at == s_at).astype(jnp.float32)
     cum = dot(lower, log_decay, precision=high)
     cum_rows = dot(cum, same, ((0,), (0,)), precision=high)
     beta_rows = dot(beta, same, ((0,), (0,)), precision=high)
+    sums[...] = cum
+    rows[0, 0:8, :] = cum_rows
+    rows[0, 8:16, :] = beta_rows
+
+    for h in range(8):
+        q_at = slice(h * 128, h * 128 + 128)
+        k_at = slice(1024 + h * 128, 1152 + h * 128)
+        q, k = act[:, q_at], act[:, k_at]
+        v = act[:, 2048 + h * 128 : 2176 + h * 128]
+        act[:, q_at] = q * lax.rsqrt(jnp.sum(q * q, axis=-1, keepdims=True) + 1e-06)
+        k = k * lax.rsqrt(jnp.sum(k * k, axis=-1, keepdims=True) + 1e-06)
+        act[:, k_at] = k
+        last = cum[63:64, h : h + 1]
+        final = jnp.exp(last)
+        tail_row = jnp.exp(last - cum_rows[h : h + 1, :]) * beta_rows[h : h + 1, :]
+        k_b = k.astype(jnp.bfloat16)
+        send_keys[0, h] = (
+            final * keys0[0, h] + dot2(split2(k.T * tail_row), k_b)
+        ).astype(jnp.bfloat16)
+        send_values[0, h] = (
+            final * values0[0, h] + dot2(split2(v.T * tail_row), k_b)
+        ).astype(jnp.bfloat16)
+
+
+HEADS_AT_ONCE = 4
+
+
+def by_request(shape):
+    return pl.BlockSpec(shape, lambda r, *_: (r,) + (0,) * (len(shape) - 1))
+
+
+def whole(shape):
+    return pl.BlockSpec(shape, lambda r, *_: (0,) * len(shape))
+
+
+STATE = (1, 8, 128, 128)
+
+
+def statistics(lengths, dest, tokens, w_gates, gain, rate, conv_weight, tail, keys0, values0, qs):
+    def by_dest(shape):
+        return pl.BlockSpec(shape, lambda r, n, d: (d[r],) + (0,) * (len(shape) - 1))
+
+    return pl.pallas_call(
+        statistics_kernel,
+        name="statistics",
+        grid_spec=pltpu.PrefetchScalarGridSpec(
+            num_scalar_prefetch=2,
+            grid=(4,),
+            in_specs=[
+                whole((256, 1024)), whole((1024, 16)), whole((1, 1024)), whole((1, 8)),
+                whole((4, 3072)), by_request((1, 3, 3072)), by_request(STATE),
+                by_request(STATE), whole((4, 1024, 256)), whole((4, 1024, 256)),
+                whole((4, 1024, 256)),
+            ],
+            out_specs=[
+                by_request((64, 3072)), by_request((64, 8)), by_request((1, 16, 64)),
+                by_dest(STATE), by_dest(STATE), by_dest((1, 3, 3072)),
+            ],
+            scratch_shapes=[
+                pltpu.VMEM((256, 1024), jnp.bfloat16),
+                pltpu.VMEM((256, 3072), jnp.bfloat16),
+                pltpu.VMEM((80, 3072), jnp.float32),
+            ],
+        ),
+        out_shape=[
+            jax.ShapeDtypeStruct((256, 3072), jnp.float32),
+            jax.ShapeDtypeStruct((256, 8), jnp.float32),
+            jax.ShapeDtypeStruct((4, 16, 64), jnp.float32),
+            jax.ShapeDtypeStruct((4, 8, 128, 128), jnp.bfloat16),
+            jax.ShapeDtypeStruct((4, 8, 128, 128), jnp.bfloat16),
+            jax.ShapeDtypeStruct((4, 3, 3072), jnp.bfloat16),
+        ],
+        compiler_params=pltpu.CompilerParams(vmem_limit_bytes=60 << 20),
+    )(lengths, dest, tokens, w_gates, gain, rate, conv_weight, tail, keys0, values0, *qs)
+
+
+def handover_copies(sent, got, sems):
+    req, peer = lax.axis_index("req"), lax.axis_index("mesh")
+    return [
+        pltpu.make_async_remote_copy(
+            src_ref=src.at[lax.rem(peer + by, 4)],
+            dst_ref=dst.at[peer],
+            send_sem=sems.at[0, by, n],
+            recv_sem=sems.at[1, by, n],
+            device_id=(req, lax.rem(peer + by, 4)),
+            device_id_type=MESH,
+        )
+        for by in range(1, 4)
+        for n, (src, dst) in enumerate(zip(sent, got))
+    ]
+
+
+def solve_kernel(
+    act, sums, rows, ridge, keys0, values0, keys, values, tails,
+    readout, got_keys, got_values, got_tails,
+    sems,
+):
+    r = pl.program_id(0)
+    req, peer = lax.axis_index("req"), lax.axis_index("mesh")
+    sent, got = (keys, values, tails), (got_keys, got_values, got_tails)
+
+    @pl.when(r == 0)
+    def _():
+        barrier = pltpu.get_barrier_semaphore()
+        for by in range(1, 4):
+            pl.semaphore_signal(
+                barrier, inc=1, device_id=(req, lax.rem(peer + by, 4)), device_id_type=MESH
+            )
+        pl.semaphore_wait(barrier, 3)
+        for copy in handover_copies(sent, got, sems):
+            copy.start()
+
+    t_at = lax.broadcasted_iota(jnp.int32, (64, 64), 0)
+    s_at = lax.broadcasted_iota(jnp.int32, (64, 64), 1)
+    causal = s_at <= t_at
+    cum = sums[...]
     carried_all = jnp.exp(cum)
-
     for first in range(0, 8, HEADS_AT_ONCE):
         heads = range(first, first + HEADS_AT_ONCE)
         states = []
@@ -386,33 +500,16 @@
             q = act[:, h * 128 : h * 128 + 128]
             k = act[:, 1024 + h * 128 : 1152 + h * 128]
             v = act[:, 2048 + h * 128 : 2176 + h * 128]
-            q = q * lax.rsqrt(jnp.sum(q * q, axis=-1, keepdims=True) + 1e-06)
-            k = k * lax.rsqrt(jnp.sum(k * k, axis=-1, keepdims=True) + 1e-06)
-            cum_col, cum_row = cum[:, h : h + 1], cum_rows[h : h + 1, :]
-            beta_row = beta_rows[h : h + 1, :]
-            spread = jnp.exp(jnp.minimum(cum_col - cum_row, 0.0))
-            weight = jnp.where(causal, spread, 0.0) * beta_row
-            last = cum[63:64, h : h + 1]
-            final = jnp.exp(last)
-            tail_row = jnp.exp(last - cum_row) * beta_row
-            k_b = k.astype(jnp.bfloat16)
-            k_t, v_t = k.T, v.T
-            start_k, start_v = keys0[0, h], values0[0, h]
-            send_keys[0, h] = (
-                final * start_k + dot2(split2(k_t * tail_row), k_b)
-            ).astype(jnp.bfloat16)
-            send_values[0, h] = (
-                final * start_v + dot2(split2(v_t * tail_row), k_b)
-            ).astype(jnp.bfloat16)
-            right = jnp.concatenate(
-                [start_k.astype(jnp.bfloat16), k_t.astype(jnp.bfloat16)], axis=1
-            )
+            spread = jnp.exp(jnp.minimum(cum[:, h : h + 1] - rows[0, h : h + 1, :], 0.0))
+            weight = jnp.where(causal, spread, 0.0) * rows[0, 8 + h : 9 + h, :]
+            k_tb = k.T.astype(jnp.bfloat16)
             states.append(
                 dict(
                     x=jnp.zeros_like(q), res=q, p=q, rr=jnp.sum(q * q, axis=-1, keepdims=True),
-                    right=right, k_b=k_b, k_tb=k_t.astype(jnp.bfloat16), v_b=v.astype(jnp.bfloat16),
-                    v0=start_v.astype(jnp.bfloat16), weight=weight,
-                    carried=carried_all[:, h : h + 1], ridge=ridge[h],
+                    right=jnp.concatenate([keys0[0, h].astype(jnp.bfloat16), k_tb], axis=1),
+                    k_b=k.astype(jnp.bfloat16), k_tb=k_tb, v_b=v.astype(jnp.bfloat16),
+                    v0=values0[0, h].astype(jnp.bfloat16), weight=weight,
+                    carried=carried_all[:, h : h + 1], ridge=ridge[:, h : h + 1],
                 )
             )
         for _ in range(ITERS):
@@ -438,105 +535,40 @@
                 start + dot2(split2(scores), s["v_b"])
             ).astype(jnp.bfloat16)
 
-
-HEADS_AT_ONCE = 4
-
-
-def mesa(lengths, dest, ridge, tokens, w_gates, gain, rate, conv_weight, tail, keys0, values0, qs):
-    def whole(shape):
-        return pl.BlockSpec(shape, lambda r, *_: (0,) * len(shape))
-
-    def by_request(shape):
-        return pl.BlockSpec(shape, lambda r, *_: (r,) + (0,) * (len(shape) - 1))
-
-    def by_dest(shape):
-        return pl.BlockSpec(shape, lambda r, n, d, *_: (d[r],) + (0,) * (len(shape) - 1))
-
-    state = (1, 8, 128, 128)
+    @pl.when(r == 3)
+    def _():
+        for by in range(1, 4):
+            source = lax.rem(peer + 4 - by, 4)
+            for n, dst in enumerate(got):
+                pltpu.make_async_remote_copy(
+                    src_ref=dst.at[source],
+                    dst_ref=dst.at[source],
+                    send_sem=sems.at[0, by, n],
+                    recv_sem=sems.at[1, by, n],
+                    device_id=(req, peer),
+                    device_id_type=MESH,
+                ).wait_recv()
+        for copy in handover_copies(sent, got, sems):
+            copy.wait_send()
+
+
+def solve(act, sums, rows, ridge, keys0, values0, own):
     return pl.pallas_call(
-        mesa_kernel,
-        name="mesa",
-        grid_spec=pltpu.PrefetchScalarGridSpec(
-            num_scalar_prefetch=3,
-            grid=(4,),
-            in_specs=[
-                whole((256, 1024)), whole((1024, 16)), whole((1, 1024)), whole((1, 8)),
-                whole((8, 1)), whole((4, 3072)), by_request((1, 3, 3072)), by_request(state),
-                by_request(state), whole((4, 1024, 256)), whole((4, 1024, 256)),
-                whole((4, 1024, 256)),
-            ],
-            out_specs=[
-                by_request((64, 1024)), by_dest(state), by_dest(state), by_dest((1, 3, 3072)),
-            ],
-            scratch_shapes=[
-                pltpu.VMEM((256, 1024), jnp.bfloat16),
-                pltpu.VMEM((256, 3072), jnp.bfloat16),
-                pltpu.VMEM((80, 3072), jnp.float32),
-                pltpu.VMEM((64, 3072), jnp.float32),
-            ],
+        solve_kernel,
+        name="solve",
+        grid=(4,),
+        in_specs=[
+            by_request((64, 3072)), by_request((64, 8)), by_request((1, 16, 64)),
+            whole((1, 8)), by_request(STATE), by_request(STATE), ANY, ANY, ANY,
+        ],
+        out_specs=[by_request((64, 1024)), ANY, ANY, ANY],
+        out_shape=[jax.ShapeDtypeStruct((256, 1024), jnp.bfloat16)]
+        + [jax.ShapeDtypeStruct(a.shape, a.dtype) for a in own],
+        scratch_shapes=[pltpu.SemaphoreType.DMA((2, 4, 3))],
+        compiler_params=pltpu.CompilerParams(
+            collective_id=1, has_side_effects=True, vmem_limit_bytes=60 << 20
         ),
-        out_shape=[
-            jax.ShapeDtypeStruct((256, 1024), jnp.bfloat16),
-            jax.ShapeDtypeStruct((4, 8, 128, 128), jnp.bfloat16),
-            jax.ShapeDtypeStruct((4, 8, 128, 128), jnp.bfloat16),
-            jax.ShapeDtypeStruct((4, 3, 3072), jnp.bfloat16),
-        ],
-        compiler_params=pltpu.CompilerParams(vmem_limit_bytes=60 << 20),
-    )(
-        lengths, dest, ridge, tokens, w_gates, gain, rate, rate.reshape(8, 1), conv_weight, tail,
-        keys0, values0, *qs,
-    )
-
-
-def handover_kernel(keys, values, tails, got_keys, got_values, got_tails, sems):
-    req, peer = lax.axis_index("req"), lax.axis_index("mesh")
-    barrier = pltpu.get_barrier_semaphore()
-    for by in range(1, 4):
-        pl.semaphore_signal(
-            barrier, inc=1, device_id=(req, lax.rem(peer + by, 4)), device_id_type=MESH
-        )
-    pl.semaphore_wait(barrier, 3)
-    copies = []
-    for by in range(1, 4):
-        other = lax.rem(peer + by, 4)
-        for n, (src, dst) in enumerate(
-            ((keys, got_keys), (values, got_values), (tails, got_tails))
-        ):
-            copy = pltpu.make_async_remote_copy(
-                src_ref=src.at[other],
-                dst_ref=dst.at[peer],
-                send_sem=sems.at[0, by, n],
-                recv_sem=sems.at[1, by, n],
-                device_id=(req, other),
-                device_id_type=MESH,
-            )
-            copy.start()
-            copies.append(copy)
-    for by in range(1, 4):
-        source = lax.rem(peer + 4 - by, 4)
-        for n, dst in enumerate((got_keys, got_values, got_tails)):
-            pltpu.make_async_remote_copy(
-                src_ref=dst.at[source],
-                dst_ref=dst.at[source],
-                send_sem=sems.at[0, by, n],
-                recv_sem=sems.at[1, by, n],
-                device_id=(req, peer),
-                device_id_type=MESH,
-            ).wait_recv()
-    for copy in copies:
-        copy.wait_send()
-
-
-def handover(keys, values, tails):
-    return pl.pallas_call(
-        handover_kernel,
-        name="handover",
-        out_shape=[jax.ShapeDtypeStruct(a.shape, a.dtype) for a in (keys, values, tails)],
-        in_specs=[ANY] * 3,
-        out_specs=[ANY] * 3,
-        scratch_shapes=[pltpu.SemaphoreType.DMA((2, 4, 3))],
-        compiler_params=pltpu.CompilerParams(collective_id=1, has_side_effects=True),
-    )(keys, values, tails)
+    )(act, sums, rows, ridge, keys0, values0, *own)
 
 
 def finish_kernel(
@@ -641,11 +673,11 @@
     me = lax.axis_index("mesh").astype(jnp.int32)
     group = all_pages[:, 0, :requests]
     slots = jnp.sum(jnp.where(group // requests == me, group % requests, 0), axis=1)
-    readout, *own = mesa(
-        lengths, page_table // requests, ridge, flat, w_gates, attn_gain[None, :],
-        decay_rate[None, :], conv_weight, conv_tail, ridge_keys, ridge_values, (qa, qb, qc),
+    act, sums, rows, *own = statistics(
+        lengths, page_table // requests, flat, w_gates, attn_gain[None, :], decay_rate[None, :],
+        conv_weight, conv_tail, ridge_keys, ridge_values, (qa, qb, qc),
     )
-    got = handover(*own)
+    readout, *got = solve(act, sums, rows, ridge[None, :], ridge_keys, ridge_values, own)
     mixed, keys, values, tails = finish(
         slots, me[None], readout, flat, ffn_gain[None, :], wo, wg, wu, wd, got, own
     )

time: 184 us -> 164 us (0.89)
  Pallas kernels: 172 us -> 153 us
    pallas_call x2, Pallas kernels: 61.8 us -> 42.6 us  [the longest x1 29 us: solve(): pl.pallas_call(solve_kernel, name='solve', grid=(4,), in_specs=[by_reques...]
    unnamed x3 -> x6, local copies, waits for them, and re-layouts: 4.74 us -> 5.54 us
where the time goes in v2:
time: 164 us
  Pallas kernels  153 us (93%)
  local copies, waits for them, and re-layouts  7.52 us (5%)
  other arithmetic  3.16 us (2%)
    pallas_call x1, Pallas kernels, gather_all(): pl.pallas_call(gather_kernel, name='gather_weights', out_shape=[block(256...  94.8 us
    pallas_call x1, Pallas kernels, solve(): pl.pallas_call(solve_kernel, name='solve', grid=(4,), in_specs=[by_reques...  29 us
    pallas_call x1, Pallas kernels, finish(): pl.pallas_call(finish_kernel, name='finish', grid_spec=pltpu.PrefetchScal...  15.2 us
    pallas_call x1, Pallas kernels, statistics(): pl.pallas_call(statistics_kernel, name='statistics', grid_spec=pltpu.Pref...  13.6 us
    unnamed x6, local copies, waits for them, and re-layouts  5.54 us

profile of v2, /device:TPU:1, one launch (start us, length us, event | category | flops | bytes accessed | tf_op | source)
XLA Modules:
  0.0 163.9 jit_solution(14903680162559462552)
XLA Ops:
  0.6 0.7 pad.6
  1.3 1.2 and_select_fusion.dest
  2.5 0.6 pad.7.pages_ref
  3.1 1.4 pad_maximum_fusion.pieces_ref
  4.4 1.6 copy.23.tail
  6.0 1.6 copy.22.w_gates
  7.6 94.8 %gather_weights.1 = (bf16[2,2,4,4,4,16,256]{6,5,4,3,2,1,0:T(8,128)(2,1)}, bf16[2,2,4,4,4,16,256]{6,5,4,3,2,1,0:T(8,128)(2,1)}, bf16[2,2,4,4,4,16,256]{6,5,4,3,2,...) custom-call(bf16[4,4,1024]{2,1,0:T(4,128)(2,1)} %pad_maximum_fusion., ...), custom_call_target="tpu_custom_call" | custom-call | tf_op jit(solution)/shard_map/gather_weights/pallas_call | solution.py:289
  102.4 0.7 slice.3
  103.1 0.6 fusion.2.slots
  103.7 13.6 %statistics.1 = (f32[256,3072]{1,0:T(8,128)}, f32[256,8]{1,0:T(8,128)}, f32[4,16,64]{2,1,0:T(8,128)}, bf16[4,8,128,128]{3,2,1,0:T(8,128)(2,1)}, bf16[4,8,128,128...) custom-call(s32[4]{0:T(128)} %lengths.1, s32[4]{0:T(128)} %and_select_fusion.dest, bf16[256,1024]{1,0:T(8,128)(2,1)} %bitcast.26, ...), custom_call_target="tpu_custom_call" | custom-call | tf_op jit(solution)/shard_map/statistics/pallas_call | solution.py:421
  117.4 29.0 %solve.1 = (bf16[256,1024]{1,0:T(8,128)(2,1)}, bf16[4,8,128,128]{3,2,1,0:T(8,128)(2,1)}, bf16[4,8,128,128]{3,2,1,0:T(8,128)(2,1)}, bf16[4,3,3072]{2,1,0:T(4,128)(2,1)}) custom-call(f32[256,3072]{1,0:T(8,128)} %get-tuple-element.31.act, f32[256,8]{1,0:T(8,128)} %get-tuple-element.32.sums, f32[4,16,64]{2,1,0:T(8,128)} %get-tuple-element.33.rows, ...), custom_call_target="tpu_custom_call" | custom-call | tf_op jit(solution)/shard_map/solve/pallas_call | solution.py:556
  146.4 0.0 copy-start
  146.4 15.2 %finish.1 = (bf16[256,1024]{1,0:T(8,128)(2,1)}, f32[4,8,128,128]{3,2,1,0:T(8,128)}, f32[4,8,128,128]{3,2,1,0:T(8,128)}, bf16[4,3,3072]{2,1,0:T(4,128)(2,1)}) custom-call(s32[4]{0:T(128)} %fusion.2.slots, s32[1]{0:T(128)} %bitcast.6.me, bf16[256,1024]{1,0:T(8,128)(2,1)} %get-tuple-element.37.readout, bf16[256,1024]{1,0:T(8,128)(2,1)} %bitcast.27, ...), custom_call_target="tpu_custom_call" | custom-call | tf_op jit(solution)/shard_map/finish/pallas_call | solution.py:631
  161.6 1.6 copy.24
  163.1 0.0 copy-done
  163.1 0.8 copy.26
Async XLA Ops:
  146.4 16.7 %copy-start = (bf16[256,1024]{1,0:T(8,128)(2,1)S(1)}, bf16[256,1024]{1,0:T(8,128)(2,1)}, u32[]{:S(2)}) copy-start(bf16[256,1024]{1,0:T(8,128)(2,1)} %get-tuple-element.37.readout) | copy-start | bytes 1572868
